TPU v7x, 32 devices: a whole 2x2x4 slice. The times are simulated.
32 devices in a mesh: src: 8 (over z, x), rcv: 4 (over y, core).
Axes of the slice: x: 2, y: 2, z: 4, core: 2. Of those that a mesh axis runs over, the one named last changes fastest.
Arguments:
- traces: bfloat16 [2, 2, 2048, 2048], P(None, None, 'src', 'rcv'), may hold values from -8 to 8
- wavelet: float32 [2, 2], replicated, may hold values from -0.3 to 0.3
Outputs:
- coeffs: float32 [2, 2, 2048, 2048], P(None, None, 'src', 'rcv')
- norms: float32 [2, 2], replicated
All inputs are finite; a program needn't handle non-finite values.
Results may differ from a plain program's by a relative error of at most 0.006.
Values may be sent and summed in bfloat16 or wider, within the bound.
A program may use at most 128 MiB of HBM per device.

v0:
```python
import math
import jax
import jax.numpy as jnp
from jax import lax
from jax.sharding import PartitionSpec as P

ITERS = 2
step_length = 0.4
shrink_fraction = 0.2


def table_block(offset, height, second, breadth, length, direction):
    left_index = offset + jnp.arange(height, dtype=jnp.int32)
    right_index = second + jnp.arange(breadth, dtype=jnp.int32)
    phase = left_index[:, None] * right_index[None, :] % length
    angle = phase.astype(jnp.float32) * (2.0 * math.pi / length)
    scale = 1.0 / math.sqrt(length)
    return jnp.stack([jnp.cos(angle) * scale, direction * (jnp.sin(angle) * scale)]).astype(
        jnp.bfloat16
    )


def complex_product(left_side, right_side, pattern, left_table, right_table):
    left_re = left_side[0] if left_table else left_side[:, 0]
    left_im = left_side[1] if left_table else left_side[:, 1]
    right_re = right_side[0] if right_table else right_side[:, 0]
    right_im = right_side[1] if right_table else right_side[:, 1]

    def single(first_op, second_op):
        return jnp.einsum(pattern, first_op, second_op, preferred_element_type=jnp.float32)

    real_part = single(left_re, right_re) - single(left_im, right_im)
    imag_part = single(left_re, right_im) + single(left_im, right_re)
    return jnp.stack([real_part, imag_part], axis=1)


def complex_scale(real_part, imag_part, values):
    return jnp.stack(
        [
            real_part * values[:, 0] - imag_part * values[:, 1],
            real_part * values[:, 1] + imag_part * values[:, 0],
        ],
        axis=1,
    )


def per_device(traces, wavelet):
    row_count = traces.shape[2]
    col_count = traces.shape[3]
    extent = row_count * lax.axis_size("src")
    row_anchor = lax.axis_index("src") * row_count
    col_anchor = lax.axis_index("rcv") * col_count
    root_scale = 1.0 / math.sqrt(extent)
    wave_re = (wavelet[:, 0] * root_scale)[:, None, None]
    wave_im = (wavelet[:, 1] * root_scale)[:, None, None]
    forward_cols = table_block(0, extent, col_anchor, col_count, extent, -1.0)
    forward_rows = table_block(row_anchor, row_count, 0, extent, extent, -1.0)
    inverse_cols = table_block(0, extent, col_anchor, col_count, extent, 1.0)
    inverse_rows = table_block(row_anchor, row_count, 0, extent, extent, 1.0)
    coeffs = jnp.zeros(traces.shape, jnp.float32)
    columns_all = lax.all_gather(traces, "src", axis=2, tiled=True)
    traces_f = traces.astype(jnp.float32)

    def row_section(table, portion):
        return complex_product(portion, table, "fmn,nc->fmc", False, True)

    def column_section(table, portion):
        return complex_product(table, portion, "mn,fnc->fmc", True, False)

    def paired(first_op, second_op):
        return jnp.einsum("fmr,fkr->fmk", first_op, second_op, preferred_element_type=jnp.float32)

    norm_list = []
    for iteration in range(ITERS):
        if iteration == 0:
            misfit = traces_f
        else:
            coeff_half = coeffs.astype(jnp.bfloat16)
            halfway = column_section(
                inverse_rows, lax.all_gather(coeff_half, "src", axis=2, tiled=True)
            ).astype(jnp.bfloat16)
            model = row_section(
                inverse_cols, lax.all_gather(halfway, "rcv", axis=3, tiled=True)
            ).astype(jnp.bfloat16)
            product = complex_product(
                lax.all_gather(model, "rcv", axis=3, tiled=True),
                columns_all,
                "fmn,fnc->fmc",
                False,
                False,
            )
            misfit = traces_f - model.astype(jnp.float32) + complex_scale(wave_re, wave_im, product)
        local_squares = jnp.sum(misfit * misfit, axis=(1, 2, 3))
        norm_list.append(jnp.sqrt(lax.psum(local_squares, ("src", "rcv"))))
        misfit_half = misfit.astype(jnp.bfloat16)
        misfit_re = misfit_half[:, 0]
        misfit_im = misfit_half[:, 1]
        column_re = columns_all[:, 0]
        column_im = columns_all[:, 1]
        back_re = paired(misfit_re, column_re) + paired(misfit_im, column_re * 0 + column_im)
        back_im = paired(misfit_im, column_re) - paired(misfit_re, column_im)
        scaled = complex_scale(wave_re, -wave_im, jnp.stack([back_re, back_im], axis=1))
        summed = lax.psum_scatter(
            scaled.astype(jnp.bfloat16), "rcv", scatter_dimension=3, tiled=True
        ).astype(jnp.float32)
        grad_half = (misfit_half.astype(jnp.float32) - summed).astype(jnp.bfloat16)
        halfway = row_section(
            forward_cols, lax.all_gather(grad_half, "rcv", axis=3, tiled=True)
        ).astype(jnp.bfloat16)
        spectrum = column_section(forward_rows, lax.all_gather(halfway, "src", axis=2, tiled=True))
        trial = coeffs + step_length * spectrum
        magnitude = jnp.sqrt(trial[:, 0] * trial[:, 0] + trial[:, 1] * trial[:, 1])
        local_peak = jnp.max(magnitude, axis=(1, 2))
        global_peak = lax.pmax(local_peak, ("src", "rcv"))
        level = shrink_fraction * global_peak[:, None, None]
        factor = jnp.maximum(1.0 - level / jnp.maximum(magnitude, level), 0.0)
        coeffs = trial * factor[:, None]
    return (coeffs, jnp.stack(norm_list))


def solution(mesh):
    in_specs = (P(None, None, "src", "rcv"), P())
    out_specs = (P(None, None, "src", "rcv"), P())
    return jax.shard_map(
        per_device, mesh=mesh, in_specs=in_specs, out_specs=out_specs, check_vma=False
    )
```

profile of v0, /device:TPU:0, one launch (start us, length us, event | category | flops | bytes accessed | tf_op | source)
XLA Modules:
  0.0 1197.7 jit_solution(8126801174571797452)
XLA Ops:
  10.5 127.4 %all-gather.9.cloned.1.call-done = bf16[2,2,2048,512]{3,2,0,1:T(8,128)(2,1)} async-done(((bf16[2,2,256,512]{3,2,0,1:T(8,128)(2,1)}), bf16[2,2,2048,512]{3,2,0,1:T(8,128)(2,1)}) %all-gather.9.cloned.1.call-update) | async-done | bytes 8388624 | tf_op jit(solution)/shard_map/all_gather | solution.py:61
  137.9 3.8 fusion.137
  142.7 3.3 fusion.138
  146.0 3.3 bitcast_add_fusion
  153.7 42.7 %reduce-scatter.3.cloned.1.call-done = bf16[2,2,256,512]{3,2,0,1:T(8,128)(2,1)} async-done(((bf16[2,2,256,2048]{3,2,0,1:T(8,128)(2,1)}), bf16[2,2,256,512]{3,2,0,1:T(8,128)(2,1)}) %reduce-scatter.3.cloned.1.call-update) | async-done | bytes 1048592 | tf_op jit(solution)/shard_map/reduce_scatter | solution.py:103
  196.4 2.5 fusion.20
  199.4 34.1 %all-gather.11.cloned.1.call-done = bf16[2,2,256,2048]{3,2,0,1:T(8,128)(2,1)} async-done(((bf16[2,2,256,512]{3,2,0,1:T(8,128)(2,1)}), bf16[2,2,256,2048]{3,2,0,1:T(8,128)(2,1)}) %all-gather.11.cloned.1.call-update) | async-done | bytes 4194320 | tf_op jit(solution)/shard_map/all_gather | solution.py:108
  233.5 17.6 %fusion.45 = f32[2,256,512]{2,1,0:T(8,128)S(1)} fusion(s32[512]{0:T(512)S(1)} %iota_add_fusion, bf16[2,2,256,2048]{3,2,0,1:T(8,128)(2,1)} %all-gather.11.cloned.1.call-done), kind=kOutput, calls=%fused_computation.87 | convolution fusion | flops 1090519040 | bytes 3147776 | tf_op jit(solution)/shard_map/fmn,nc->fmc/dot_general | solution.py:30
  251.1 15.9 %fusion.47 = f32[2,256,512]{2,1,0:T(8,128)S(1)} fusion(s32[512]{0:T(512)S(1)} %iota_add_fusion, bf16[2,2,256,2048]{3,2,0,1:T(8,128)(2,1)S(1)} %copy-done.13), kind=kOutput, calls=%fused_computation.88 | convolution fusion | flops 1090519040 | bytes 3147776 | tf_op jit(solution)/shard_map/fmn,nc->fmc/dot_general | solution.py:30
  266.9 16.4 %fusion.124 = bf16[2,1,256,512]{3,2,0,1:T(8,128)(2,1)S(1)} fusion(f32[2,256,512]{2,1,0:T(8,128)S(1)} %fusion.45, s32[512]{0:T(512)S(1)} %iota_add_fusion, bf16[2,2,256,2048]{3,2,0,1:T(8,128)(2,1)S(1)} %copy-done.13), kind=kOutput, calls=%fused_computation.129 | convolution fusion | flops 1091043328 | bytes 3672064 | tf_op jit(solution)/shard_map/fmn,nc->fmc/dot_general | solution.py:30
  283.3 16.6 %fusion.121 = bf16[2,1,256,512]{3,2,0,1:T(8,128)(2,1)S(1)} fusion(f32[2,256,512]{2,1,0:T(8,128)S(1)} %fusion.47, s32[512]{0:T(512)S(1)} %iota_add_fusion, bf16[2,2,256,2048]{3,2,0,1:T(8,128)(2,1)S(1)} %copy-done.13), kind=kOutput, calls=%fused_computation.128 | convolution fusion | flops 1091043328 | bytes 3672064 | tf_op jit(solution)/shard_map/fmn,nc->fmc/dot_general | solution.py:30
  301.1 124.5 %all-gather.13.cloned.1.call-done = bf16[2,2,2048,512]{3,2,0,1:T(8,128)(2,1)} async-done(((bf16[2,2,256,512]{3,2,0,1:T(8,128)(2,1)}), bf16[2,2,2048,512]{3,2,0,1:T(8,128)(2,1)}) %all-gather.13.cloned.1.call-update) | async-done | bytes 8388624 | tf_op jit(solution)/shard_map/all_gather | solution.py:110
  425.6 10.8 fusion.6
  436.4 8.5 fusion.7
  444.9 8.7 fusion.92
  453.7 8.4 fusion.90
  463.6 38.3 %pmax.14 = f32[2]{0:T(128)S(1)} all-reduce(f32[2]{0:T(128)S(1)} %fusion.160), channel_id=1, replica_groups=mesh['src'=8,'rcv'=4] {'src','rcv'}, use_global_device_ids=true, to_apply=%region_2.3 | all-reduce | flops 2 | bytes 16 | tf_op jit(solution)/shard_map/pmax | solution.py:114
  503.4 2.8 multiply_convert_fusion.6
  506.5 125.6 %all-gather.15.cloned.1.call-done = bf16[2,2,2048,512]{2,3,0,1:T(8,128)(2,1)} async-done(((bf16[2,2,256,512]{2,3,0,1:T(8,128)(2,1)}), bf16[2,2,2048,512]{2,3,0,1:T(8,128)(2,1)}) %all-gather.15.cloned.1.call-update) | async-done | bytes 8388624 | tf_op jit(solution)/shard_map/all_gather | solution.py:80
  632.0 11.0 fusion.10
  643.0 8.7 fusion.11
  651.8 9.0 fusion.134
  660.7 8.6 fusion.133
  670.6 32.6 %all-gather.17.cloned.1.call-done = bf16[2,2,256,2048]{2,3,0,1:T(8,128)(2,1)} async-done(((bf16[2,2,256,512]{2,3,0,1:T(8,128)(2,1)}), bf16[2,2,256,2048]{2,3,0,1:T(8,128)(2,1)}) %all-gather.17.cloned.1.call-update) | async-done | bytes 4194320 | tf_op jit(solution)/shard_map/all_gather | solution.py:83
  703.2 18.5 %fusion.41 = f32[2,256,512]{2,1,0:T(8,128)S(1)} fusion(s32[512]{0:T(512)S(1)} %iota_add_fusion, bf16[2,2,256,2048]{2,3,0,1:T(8,128)(2,1)} %all-gather.17.cloned.1.call-done), kind=kOutput, calls=%fused_computation.85 | convolution fusion | flops 1090519040 | bytes 3147776 | tf_op jit(solution)/shard_map/fmn,nc->fmc/dot_general | solution.py:30
  721.7 16.9 %fusion.43 = f32[2,256,512]{2,1,0:T(8,128)S(1)} fusion(s32[512]{0:T(512)S(1)} %iota_add_fusion, bf16[2,2,256,2048]{2,3,0,1:T(8,128)(2,1)S(1)} %copy-done.16), kind=kOutput, calls=%fused_computation.86 | convolution fusion | flops 1090519040 | bytes 3147776 | tf_op jit(solution)/shard_map/fmn,nc->fmc/dot_general | solution.py:30
  738.6 17.2 %fusion.118 = bf16[2,1,256,512]{3,2,0,1:T(8,128)(2,1)S(1)} fusion(f32[2,256,512]{2,1,0:T(8,128)S(1)} %fusion.41, s32[512]{0:T(512)S(1)} %iota_add_fusion, bf16[2,2,256,2048]{2,3,0,1:T(8,128)(2,1)S(1)} %copy-done.16), kind=kOutput, calls=%fused_computation.127 | convolution fusion | flops 1091043328 | bytes 3672064 | tf_op jit(solution)/shard_map/fmn,nc->fmc/dot_general | solution.py:30
  755.8 16.8 %fusion.115 = bf16[2,1,256,512]{3,2,0,1:T(8,128)(2,1)S(1)} fusion(f32[2,256,512]{2,1,0:T(8,128)S(1)} %fusion.43, s32[512]{0:T(512)S(1)} %iota_add_fusion, bf16[2,2,256,2048]{2,3,0,1:T(8,128)(2,1)S(1)} %copy-done.16), kind=kOutput, calls=%fused_computation.126 | convolution fusion | flops 1091043328 | bytes 3672064 | tf_op jit(solution)/shard_map/fmn,nc->fmc/dot_general | solution.py:30
  773.8 34.6 %all-gather.19.cloned.1.call-done = bf16[2,2,256,2048]{3,2,0,1:T(8,128)(2,1)} async-done(((bf16[2,2,256,512]{3,2,0,1:T(8,128)(2,1)}), bf16[2,2,256,2048]{3,2,0,1:T(8,128)(2,1)}) %all-gather.19.cloned.1.call-update) | async-done | bytes 4194320 | tf_op jit(solution)/shard_map/all_gather | solution.py:86
  808.4 4.2 fusion.63
  812.6 3.6 fusion.62
  816.2 3.6 fusion.93
  826.0 3.6 fusion.31
  829.6 4.5 pad_maximum_fusion.1
  834.2 44.5 %reduce-scatter.5.cloned.1.call-done = bf16[2,2,256,512]{3,2,0,1:T(8,128)(2,1)} async-done(((bf16[2,2,256,2048]{3,2,0,1:T(8,128)(2,1)}), bf16[2,2,256,512]{3,2,0,1:T(8,128)(2,1)}) %reduce-scatter.5.cloned.1.call-update) | async-done | bytes 1048592 | tf_op jit(solution)/shard_map/reduce_scatter | solution.py:103
  881.6 34.2 %all-gather.21.cloned.1.call-done = bf16[2,2,256,2048]{3,2,0,1:T(8,128)(2,1)} async-done(((bf16[2,2,256,512]{3,2,0,1:T(8,128)(2,1)}), bf16[2,2,256,2048]{3,2,0,1:T(8,128)(2,1)}) %all-gather.21.cloned.1.call-update) | async-done | bytes 4194320 | tf_op jit(solution)/shard_map/all_gather | solution.py:108
  915.8 17.6 %fusion.37 = f32[2,256,512]{2,1,0:T(8,128)S(1)} fusion(s32[512]{0:T(512)S(1)} %iota_add_fusion, bf16[2,2,256,2048]{3,2,0,1:T(8,128)(2,1)} %all-gather.21.cloned.1.call-done), kind=kOutput, calls=%fused_computation.83 | convolution fusion | flops 1090519040 | bytes 3147776 | tf_op jit(solution)/shard_map/fmn,nc->fmc/dot_general | solution.py:30
  933.4 15.9 %fusion.39 = f32[2,256,512]{2,1,0:T(8,128)S(1)} fusion(s32[512]{0:T(512)S(1)} %iota_add_fusion, bf16[2,2,256,2048]{3,2,0,1:T(8,128)(2,1)S(1)} %copy-done.15), kind=kOutput, calls=%fused_computation.84 | convolution fusion | flops 1090519040 | bytes 3147776 | tf_op jit(solution)/shard_map/fmn,nc->fmc/dot_general | solution.py:30
  949.2 16.4 %fusion.130 = bf16[2,1,256,512]{3,2,0,1:T(8,128)(2,1)S(1)} fusion(f32[2,256,512]{2,1,0:T(8,128)S(1)} %fusion.37, s32[512]{0:T(512)S(1)} %iota_add_fusion, bf16[2,2,256,2048]{3,2,0,1:T(8,128)(2,1)S(1)} %copy-done.15), kind=kOutput, calls=%fused_computation.131 | convolution fusion | flops 1091043328 | bytes 3672064 | tf_op jit(solution)/shard_map/fmn,nc->fmc/dot_general | solution.py:30
  965.6 17.0 %fusion.127 = bf16[2,1,256,512]{3,2,0,1:T(8,128)(2,1)S(1)} fusion(f32[2,256,512]{2,1,0:T(8,128)S(1)} %fusion.39, s32[512]{0:T(512)S(1)} %iota_add_fusion, bf16[2,2,256,2048]{3,2,0,1:T(8,128)(2,1)S(1)} %copy-done.15), kind=kOutput, calls=%fused_computation.130 | convolution fusion | flops 1091043328 | bytes 3672064 | tf_op jit(solution)/shard_map/fmn,nc->fmc/dot_general | solution.py:30
  983.8 42.2 %all-reduce = (f32[2]{0:T(128)S(1)}, f32[2]{0:T(128)S(1)}) all-reduce(f32[2]{0:T(128)S(1)} %get-tuple-element.5, f32[2]{0:T(128)S(1)} %get-tuple-element.4), channel_id=1, replica_groups=mesh['src'=8,'rcv'=4] {'src','rcv'}, use_global_device_ids=true, to_apply=%region_9.10 | all-reduce | flops 4 | bytes 32 | tf_op jit(solution)/shard_map/psum | solution.py:94
  1025.9 83.5 %all-gather.23.cloned.1.call-done = bf16[2,2,2048,512]{3,2,0,1:T(8,128)(2,1)} async-done(((bf16[2,2,256,512]{3,2,0,1:T(8,128)(2,1)}), bf16[2,2,2048,512]{3,2,0,1:T(8,128)(2,1)}) %all-gather.23.cloned.1.call-update) | async-done | bytes 8388624 | tf_op jit(solution)/shard_map/all_gather | solution.py:110
  1109.4 10.8 fusion.14
  1120.2 8.5 fusion.15
  1128.7 8.6 fusion.86
  1137.3 8.4 fusion.84
  1147.4 38.3 %pmax.15 = f32[2]{0:T(128)S(1)} all-reduce(f32[2]{0:T(128)S(1)} %fusion.161), channel_id=1, replica_groups=mesh['src'=8,'rcv'=4] {'src','rcv'}, use_global_device_ids=true, to_apply=%region_5.6 | all-reduce | flops 2 | bytes 16 | tf_op jit(solution)/shard_map/pmax | solution.py:114
  1186.2 2.6 broadcast_multiply_fusion
  (87 shorter events, 30.1 us)
Async XLA Ops:
  7.2 130.8 %all-gather.9.cloned.1.call-start = ((), (), s32[]{:S(2)}) async-start(), calls=%async_computation.2 | async-start | bytes 9437184 | tf_op jit(solution)/shard_map/all_gather | solution.py:61
  9.5 132.3 %copy-start.1 = (bf16[2,2,256,512]{3,2,1,0:T(8,128)(2,1)S(1)}, bf16[2,2,256,512]{3,2,1,0:T(8,128)(2,1)}, u32[]{:S(2)}) copy-start(bf16[2,2,256,512]{3,2,1,0:T(8,128)(2,1)} %param.2) | copy-start | bytes 3145732
  9.5 186.9 %reduce-scatter.3.cloned.1.call-start = ((), (), s32[]{:S(2)}) async-start(), calls=%async_computation.3 | async-start | bytes 5242880 | tf_op jit(solution)/shard_map/reduce_scatter | solution.py:103
  137.9 4.8 copy-start
  153.6 79.9 %all-gather.11.cloned.1.call-start = ((), (), s32[]{:S(2)}) async-start(), calls=%async_computation.4 | async-start | bytes 5242880 | tf_op jit(solution)/shard_map/all_gather | solution.py:108
  198.9 226.7 %all-gather.13.cloned.1.call-start = ((), (), s32[]{:S(2)}) async-start(), calls=%async_computation.5 | async-start | bytes 9437184 | tf_op jit(solution)/shard_map/all_gather | solution.py:110
  233.5 17.6 %copy-start.13 = (bf16[2,2,256,2048]{3,2,0,1:T(8,128)(2,1)S(1)}, bf16[2,2,256,2048]{3,2,0,1:T(8,128)(2,1)}, u32[]{:S(2)}) copy-start(bf16[2,2,256,2048]{3,2,0,1:T(8,128)(2,1)} %all-gather.11.cloned.1.call-done) | copy-start | bytes 12582916
  301.0 331.0 %all-gather.15.cloned.1.call-start = ((), (), s32[]{:S(2)}) async-start(), calls=%async_computation.6 | async-start | bytes 9437184 | tf_op jit(solution)/shard_map/all_gather | solution.py:80
  425.6 10.8 copy-start.10
  453.7 8.4 copy-start.4
  462.1 1.0 copy-start.6
  502.4 1.0 copy-start.2
  506.2 197.0 %all-gather.17.cloned.1.call-start = ((), (), s32[]{:S(2)}) async-start(), calls=%async_computation.7 | async-start | bytes 5242880 | tf_op jit(solution)/shard_map/all_gather | solution.py:83
  632.0 11.0 copy-start.12
  670.4 138.0 %all-gather.19.cloned.1.call-start = ((), (), s32[]{:S(2)}) async-start(), calls=%async_computation.8 | async-start | bytes 5242880 | tf_op jit(solution)/shard_map/all_gather | solution.py:86
  703.2 18.5 %copy-start.16 = (bf16[2,2,256,2048]{2,3,0,1:T(8,128)(2,1)S(1)}, bf16[2,2,256,2048]{2,3,0,1:T(8,128)(2,1)}, u32[]{:S(2)}) copy-start(bf16[2,2,256,2048]{2,3,0,1:T(8,128)(2,1)} %all-gather.17.cloned.1.call-done) | copy-start | bytes 12582916
  773.8 104.9 %reduce-scatter.5.cloned.1.call-start = ((), (), s32[]{:S(2)}) async-start(), calls=%async_computation.9 | async-start | bytes 5242880 | tf_op jit(solution)/shard_map/reduce_scatter | solution.py:103
  808.4 4.2 copy-start.14
  812.6 7.2 slice-start
  816.2 3.6 slice-start.1
  834.1 81.7 %all-gather.21.cloned.1.call-start = ((), (), s32[]{:S(2)}) async-start(), calls=%async_computation.10 | async-start | bytes 5242880 | tf_op jit(solution)/shard_map/all_gather | solution.py:108
  881.2 228.2 %all-gather.23.cloned.1.call-start = ((), (), s32[]{:S(2)}) async-start(), calls=%async_computation.11 | async-start | bytes 9437184 | tf_op jit(solution)/shard_map/all_gather | solution.py:110
  915.8 17.6 %copy-start.15 = (bf16[2,2,256,2048]{3,2,0,1:T(8,128)(2,1)S(1)}, bf16[2,2,256,2048]{3,2,0,1:T(8,128)(2,1)}, u32[]{:S(2)}) copy-start(bf16[2,2,256,2048]{3,2,0,1:T(8,128)(2,1)} %all-gather.21.cloned.1.call-done) | copy-start | bytes 12582916
  1109.4 10.8 copy-start.11
  1137.3 8.5 copy-start.8
  1137.3 8.5 copy-start.3
  1137.3 8.5 copy-start.5
  1137.3 8.5 copy-start.7
  1145.8 1.0 copy-start.9
Sparse Core Ops, SparseCore 0:
  10.7 127.1 all-gather.8
  153.7 42.5 reduce-scatter.2
  199.0 34.4 all-gather.10
  301.1 124.4 all-gather.12
  506.4 125.6 all-gather.14
  670.5 32.6 all-gather.16
  773.9 34.4 all-gather.18
  834.3 44.3 reduce-scatter.4
  881.3 34.4 all-gather.20
  983.9 125.4 all-gather.22
where the time goes:
time: 1200 us
  waiting for transfers between devices  684 us (57%)
  matrix products  345 us (29%)
  blocking collectives  119 us (10%)
  other arithmetic  26.4 us (2%)
  between operations  14.9 us (1%)
    dot_general x28, matrix products, single(): jnp.einsum(pattern, first_op, second_op, preferred_element_type=jnp.float32)  325 us
    all_gather x2, waiting for transfers between devices, per_device(): lax.all_gather(halfway, 'src', axis=2, tiled=True)  208 us
    all_gather x1, waiting for transfers between devices, per_device(): columns_all = lax.all_gather(traces, 'src', axis=2, tiled=True)  127 us
    all_gather x1, waiting for transfers between devices, per_device(): lax.all_gather(coeff_half, 'src', axis=2, tiled=True)  126 us
    reduce_scatter x2, waiting for transfers between devices, per_device(): lax.psum_scatter(scaled.astype(jnp.bfloat16), 'rcv', scatter_dimension=3,...  87.2 us
    pmax x2, blocking collectives, per_device(): global_peak = lax.pmax(local_peak, ('src', 'rcv'))  76.6 us
    all_gather x2, waiting for transfers between devices, per_device(): lax.all_gather(grad_half, 'rcv', axis=3, tiled=True)  68.3 us
    psum x1, blocking collectives, per_device(): norm_list.append(jnp.sqrt(lax.psum(local_squares, ('src', 'rcv'))))  42.2 us
  transfers between devices with their start and end apart: 10, of which 10 were waited for; matrix products, arithmetic and copies ran while one was open for 0% of the time, Pallas kernels for 0%

commit v1 on v0

--- a/solution.py
+++ b/solution.py
@@ -58,7 +58,8 @@
     inverse_cols = table_block(0, extent, col_anchor, col_count, extent, 1.0)
     inverse_rows = table_block(row_anchor, row_count, 0, extent, extent, 1.0)
     coeffs = jnp.zeros(traces.shape, jnp.float32)
-    columns_all = lax.all_gather(traces, "src", axis=2, tiled=True)
+    tall = lax.all_gather(traces, "src")
+    columns_all = jnp.concatenate(tall, axis=2)
     traces_f = traces.astype(jnp.float32)
 
     def row_section(table, portion):

time: 1200 us -> 1210 us (level)
  no operation moved by 1% of the time
where the time goes in v1:
time: 1210 us; the launch traced here: 1200 us
  waiting for transfers between devices  685 us (57%)
  matrix products  345 us (29%)
  blocking collectives  119 us (10%)
  other arithmetic  24.5 us (2%)
  between operations  14.8 us (1%)
  local copies, waits for them, and re-layouts  12.6 us (1%)
    dot_general x28, matrix products, single(): jnp.einsum(pattern, first_op, second_op, preferred_element_type=jnp.float32)  323 us
    all_gather x2, waiting for transfers between devices, per_device(): lax.all_gather(halfway, 'src', axis=2, tiled=True)  208 us
    all_gather x1, waiting for transfers between devices, per_device(): tall = lax.all_gather(traces, 'src')  128 us
    all_gather x1, waiting for transfers between devices, per_device(): lax.all_gather(coeff_half, 'src', axis=2, tiled=True)  126 us
    reduce_scatter x2, waiting for transfers between devices, per_device(): lax.psum_scatter(scaled.astype(jnp.bfloat16), 'rcv', scatter_dimension=3,...  87.2 us
    pmax x2, blocking collectives, per_device(): global_peak = lax.pmax(local_peak, ('src', 'rcv'))  76.6 us
    all_gather x2, waiting for transfers between devices, per_device(): lax.all_gather(grad_half, 'rcv', axis=3, tiled=True)  68.2 us
    psum x1, blocking collectives, per_device(): norm_list.append(jnp.sqrt(lax.psum(local_squares, ('src', 'rcv'))))  42.2 us
  transfers between devices with their start and end apart: 10, of which 10 were waited for; matrix products, arithmetic and copies ran while one was open for 0% of the time, Pallas kernels for 0%

profile of v1, /device:TPU:0, one launch (start us, length us, event | category | flops | bytes accessed | tf_op | source)
XLA Modules:
  0.0 1202.5 jit_solution(2727884339384674448)
XLA Ops:
  8.9 128.4 %all-gather.24.cloned.1.call-done = bf16[16,2,256,512]{3,2,1,0:T(8,128)(2,1)} async-done(((bf16[2,2,256,512]{3,2,1,0:T(8,128)(2,1)}), bf16[16,2,256,512]{3,2,1,0:T(8,128)(2,1)}) %all-gather.24.cloned.1.call-update) | async-done | bytes 8388624 | tf_op jit(solution)/shard_map/all_gather | solution.py:61
  137.3 7.6 copy.24
  144.9 3.6 fusion.137
  149.6 3.3 fusion.138
  152.8 3.3 bitcast_add_fusion
  160.5 42.7 %reduce-scatter.3.cloned.1.call-done = bf16[2,2,256,512]{3,2,0,1:T(8,128)(2,1)} async-done(((bf16[2,2,256,2048]{3,2,0,1:T(8,128)(2,1)}), bf16[2,2,256,512]{3,2,0,1:T(8,128)(2,1)}) %reduce-scatter.3.cloned.1.call-update) | async-done | bytes 1048592 | tf_op jit(solution)/shard_map/reduce_scatter | solution.py:104
  206.2 34.1 %all-gather.10.cloned.1.call-done = bf16[2,2,256,2048]{3,2,0,1:T(8,128)(2,1)} async-done(((bf16[2,2,256,512]{3,2,0,1:T(8,128)(2,1)}), bf16[2,2,256,2048]{3,2,0,1:T(8,128)(2,1)}) %all-gather.10.cloned.1.call-update) | async-done | bytes 4194320 | tf_op jit(solution)/shard_map/all_gather | solution.py:109
  240.3 17.6 %fusion.45 = f32[2,256,512]{2,1,0:T(8,128)S(1)} fusion(s32[512]{0:T(512)S(1)} %iota_add_fusion, bf16[2,2,256,2048]{3,2,0,1:T(8,128)(2,1)} %all-gather.10.cloned.1.call-done), kind=kOutput, calls=%fused_computation.87 | convolution fusion | flops 1090519040 | bytes 3147776 | tf_op jit(solution)/shard_map/fmn,nc->fmc/dot_general | solution.py:30
  257.9 15.9 %fusion.47 = f32[2,256,512]{2,1,0:T(8,128)S(1)} fusion(s32[512]{0:T(512)S(1)} %iota_add_fusion, bf16[2,2,256,2048]{3,2,0,1:T(8,128)(2,1)S(1)} %copy-done.13), kind=kOutput, calls=%fused_computation.88 | convolution fusion | flops 1090519040 | bytes 3147776 | tf_op jit(solution)/shard_map/fmn,nc->fmc/dot_general | solution.py:30
  273.7 16.4 %fusion.124 = bf16[2,1,256,512]{3,2,0,1:T(8,128)(2,1)S(1)} fusion(f32[2,256,512]{2,1,0:T(8,128)S(1)} %fusion.45, s32[512]{0:T(512)S(1)} %iota_add_fusion, bf16[2,2,256,2048]{3,2,0,1:T(8,128)(2,1)S(1)} %copy-done.13), kind=kOutput, calls=%fused_computation.129 | convolution fusion | flops 1091043328 | bytes 3672064 | tf_op jit(solution)/shard_map/fmn,nc->fmc/dot_general | solution.py:30
  290.1 16.6 %fusion.121 = bf16[2,1,256,512]{3,2,0,1:T(8,128)(2,1)S(1)} fusion(f32[2,256,512]{2,1,0:T(8,128)S(1)} %fusion.47, s32[512]{0:T(512)S(1)} %iota_add_fusion, bf16[2,2,256,2048]{3,2,0,1:T(8,128)(2,1)S(1)} %copy-done.13), kind=kOutput, calls=%fused_computation.128 | convolution fusion | flops 1091043328 | bytes 3672064 | tf_op jit(solution)/shard_map/fmn,nc->fmc/dot_general | solution.py:30
  307.9 124.5 %all-gather.12.cloned.1.call-done = bf16[2,2,2048,512]{3,2,0,1:T(8,128)(2,1)} async-done(((bf16[2,2,256,512]{3,2,0,1:T(8,128)(2,1)}), bf16[2,2,2048,512]{3,2,0,1:T(8,128)(2,1)}) %all-gather.12.cloned.1.call-update) | async-done | bytes 8388624 | tf_op jit(solution)/shard_map/all_gather | solution.py:111
  432.4 10.8 fusion.6
  443.2 8.5 fusion.7
  451.7 8.7 fusion.92
  460.5 8.4 fusion.90
  470.4 38.3 %pmax.14 = f32[2]{0:T(128)S(1)} all-reduce(f32[2]{0:T(128)S(1)} %fusion.160), channel_id=1, replica_groups=mesh['src'=8,'rcv'=4] {'src','rcv'}, use_global_device_ids=true, to_apply=%region_2.3 | all-reduce | flops 2 | bytes 16 | tf_op jit(solution)/shard_map/pmax | solution.py:115
  510.3 2.8 multiply_convert_fusion.6
  513.3 125.6 %all-gather.14.cloned.1.call-done = bf16[2,2,2048,512]{2,3,0,1:T(8,128)(2,1)} async-done(((bf16[2,2,256,512]{2,3,0,1:T(8,128)(2,1)}), bf16[2,2,2048,512]{2,3,0,1:T(8,128)(2,1)}) %all-gather.14.cloned.1.call-update) | async-done | bytes 8388624 | tf_op jit(solution)/shard_map/all_gather | solution.py:81
  638.9 11.0 fusion.10
  649.9 8.7 fusion.11
  658.6 9.0 fusion.134
  667.6 8.6 fusion.133
  677.6 32.6 %all-gather.16.cloned.1.call-done = bf16[2,2,256,2048]{2,3,0,1:T(8,128)(2,1)} async-done(((bf16[2,2,256,512]{2,3,0,1:T(8,128)(2,1)}), bf16[2,2,256,2048]{2,3,0,1:T(8,128)(2,1)}) %all-gather.16.cloned.1.call-update) | async-done | bytes 4194320 | tf_op jit(solution)/shard_map/all_gather | solution.py:84
  710.1 18.5 %fusion.41 = f32[2,256,512]{2,1,0:T(8,128)S(1)} fusion(s32[512]{0:T(512)S(1)} %iota_add_fusion, bf16[2,2,256,2048]{2,3,0,1:T(8,128)(2,1)} %all-gather.16.cloned.1.call-done), kind=kOutput, calls=%fused_computation.85 | convolution fusion | flops 1090519040 | bytes 3147776 | tf_op jit(solution)/shard_map/fmn,nc->fmc/dot_general | solution.py:30
  728.6 16.9 %fusion.43 = f32[2,256,512]{2,1,0:T(8,128)S(1)} fusion(s32[512]{0:T(512)S(1)} %iota_add_fusion, bf16[2,2,256,2048]{2,3,0,1:T(8,128)(2,1)S(1)} %copy-done.16), kind=kOutput, calls=%fused_computation.86 | convolution fusion | flops 1090519040 | bytes 3147776 | tf_op jit(solution)/shard_map/fmn,nc->fmc/dot_general | solution.py:30
  745.5 17.2 %fusion.118 = bf16[2,1,256,512]{3,2,0,1:T(8,128)(2,1)S(1)} fusion(f32[2,256,512]{2,1,0:T(8,128)S(1)} %fusion.41, s32[512]{0:T(512)S(1)} %iota_add_fusion, bf16[2,2,256,2048]{2,3,0,1:T(8,128)(2,1)S(1)} %copy-done.16), kind=kOutput, calls=%fused_computation.127 | convolution fusion | flops 1091043328 | bytes 3672064 | tf_op jit(solution)/shard_map/fmn,nc->fmc/dot_general | solution.py:30
  762.8 16.8 %fusion.115 = bf16[2,1,256,512]{3,2,0,1:T(8,128)(2,1)S(1)} fusion(f32[2,256,512]{2,1,0:T(8,128)S(1)} %fusion.43, s32[512]{0:T(512)S(1)} %iota_add_fusion, bf16[2,2,256,2048]{2,3,0,1:T(8,128)(2,1)S(1)} %copy-done.16), kind=kOutput, calls=%fused_computation.126 | convolution fusion | flops 1091043328 | bytes 3672064 | tf_op jit(solution)/shard_map/fmn,nc->fmc/dot_general | solution.py:30
  780.8 34.6 %all-gather.18.cloned.1.call-done = bf16[2,2,256,2048]{3,2,0,1:T(8,128)(2,1)} async-done(((bf16[2,2,256,512]{3,2,0,1:T(8,128)(2,1)}), bf16[2,2,256,2048]{3,2,0,1:T(8,128)(2,1)}) %all-gather.18.cloned.1.call-update) | async-done | bytes 4194320 | tf_op jit(solution)/shard_map/all_gather | solution.py:87
  815.4 4.2 fusion.63
  819.6 3.6 fusion.62
  828.2 3.2 fusion.136
  832.7 3.9 fusion.31
  838.9 44.5 %reduce-scatter.5.cloned.1.call-done = bf16[2,2,256,512]{3,2,0,1:T(8,128)(2,1)} async-done(((bf16[2,2,256,2048]{3,2,0,1:T(8,128)(2,1)}), bf16[2,2,256,512]{3,2,0,1:T(8,128)(2,1)}) %reduce-scatter.5.cloned.1.call-update) | async-done | bytes 1048592 | tf_op jit(solution)/shard_map/reduce_scatter | solution.py:104
  883.4 2.5 subtract_convert_fusion.2
  886.4 34.2 %all-gather.20.cloned.1.call-done = bf16[2,2,256,2048]{3,2,0,1:T(8,128)(2,1)} async-done(((bf16[2,2,256,512]{3,2,0,1:T(8,128)(2,1)}), bf16[2,2,256,2048]{3,2,0,1:T(8,128)(2,1)}) %all-gather.20.cloned.1.call-update) | async-done | bytes 4194320 | tf_op jit(solution)/shard_map/all_gather | solution.py:109
  920.6 17.6 %fusion.37 = f32[2,256,512]{2,1,0:T(8,128)S(1)} fusion(s32[512]{0:T(512)S(1)} %iota_add_fusion, bf16[2,2,256,2048]{3,2,0,1:T(8,128)(2,1)} %all-gather.20.cloned.1.call-done), kind=kOutput, calls=%fused_computation.83 | convolution fusion | flops 1090519040 | bytes 3147776 | tf_op jit(solution)/shard_map/fmn,nc->fmc/dot_general | solution.py:30
  938.2 15.9 %fusion.39 = f32[2,256,512]{2,1,0:T(8,128)S(1)} fusion(s32[512]{0:T(512)S(1)} %iota_add_fusion, bf16[2,2,256,2048]{3,2,0,1:T(8,128)(2,1)S(1)} %copy-done.15), kind=kOutput, calls=%fused_computation.84 | convolution fusion | flops 1090519040 | bytes 3147776 | tf_op jit(solution)/shard_map/fmn,nc->fmc/dot_general | solution.py:30
  954.0 16.4 %fusion.130 = bf16[2,1,256,512]{3,2,0,1:T(8,128)(2,1)S(1)} fusion(f32[2,256,512]{2,1,0:T(8,128)S(1)} %fusion.37, s32[512]{0:T(512)S(1)} %iota_add_fusion, bf16[2,2,256,2048]{3,2,0,1:T(8,128)(2,1)S(1)} %copy-done.15), kind=kOutput, calls=%fused_computation.131 | convolution fusion | flops 1091043328 | bytes 3672064 | tf_op jit(solution)/shard_map/fmn,nc->fmc/dot_general | solution.py:30
  970.4 17.0 %fusion.127 = bf16[2,1,256,512]{3,2,0,1:T(8,128)(2,1)S(1)} fusion(f32[2,256,512]{2,1,0:T(8,128)S(1)} %fusion.39, s32[512]{0:T(512)S(1)} %iota_add_fusion, bf16[2,2,256,2048]{3,2,0,1:T(8,128)(2,1)S(1)} %copy-done.15), kind=kOutput, calls=%fused_computation.130 | convolution fusion | flops 1091043328 | bytes 3672064 | tf_op jit(solution)/shard_map/fmn,nc->fmc/dot_general | solution.py:30
  988.6 42.2 %all-reduce = (f32[2]{0:T(128)S(1)}, f32[2]{0:T(128)S(1)}) all-reduce(f32[2]{0:T(128)S(1)} %get-tuple-element.7, f32[2]{0:T(128)S(1)} %get-tuple-element.6), channel_id=1, replica_groups=mesh['src'=8,'rcv'=4] {'src','rcv'}, use_global_device_ids=true, to_apply=%region_9.10 | all-reduce | flops 4 | bytes 32 | tf_op jit(solution)/shard_map/psum | solution.py:95
  1030.8 83.5 %all-gather.22.cloned.1.call-done = bf16[2,2,2048,512]{3,2,0,1:T(8,128)(2,1)} async-done(((bf16[2,2,256,512]{3,2,0,1:T(8,128)(2,1)}), bf16[2,2,2048,512]{3,2,0,1:T(8,128)(2,1)}) %all-gather.22.cloned.1.call-update) | async-done | bytes 8388624 | tf_op jit(solution)/shard_map/all_gather | solution.py:111
  1114.3 10.8 fusion.14
  1125.1 8.5 fusion.15
  1133.6 8.6 fusion.86
  1142.2 8.4 fusion.84
  1152.2 38.3 %pmax.15 = f32[2]{0:T(128)S(1)} all-reduce(f32[2]{0:T(128)S(1)} %fusion.161), channel_id=1, replica_groups=mesh['src'=8,'rcv'=4] {'src','rcv'}, use_global_device_ids=true, to_apply=%region_5.6 | all-reduce | flops 2 | bytes 16 | tf_op jit(solution)/shard_map/pmax | solution.py:115
  1191.1 2.6 broadcast_multiply_fusion
  (87 shorter events, 31.2 us)
Async XLA Ops:
  7.2 130.2 %all-gather.24.cloned.1.call-start = ((), (), s32[]{:S(2)}) async-start(), calls=%async_computation.11 | async-start | bytes 9437184 | tf_op jit(solution)/shard_map/all_gather | solution.py:61
  7.9 195.3 %reduce-scatter.3.cloned.1.call-start = ((), (), s32[]{:S(2)}) async-start(), calls=%async_computation.2 | async-start | bytes 5242880 | tf_op jit(solution)/shard_map/reduce_scatter | solution.py:104
  137.3 7.6 copy-start.1
  144.9 4.6 copy-start
  160.4 79.8 %all-gather.10.cloned.1.call-start = ((), (), s32[]{:S(2)}) async-start(), calls=%async_computation.3 | async-start | bytes 5242880 | tf_op jit(solution)/shard_map/all_gather | solution.py:109
  205.7 226.7 %all-gather.12.cloned.1.call-start = ((), (), s32[]{:S(2)}) async-start(), calls=%async_computation.4 | async-start | bytes 9437184 | tf_op jit(solution)/shard_map/all_gather | solution.py:111
  240.3 17.6 %copy-start.13 = (bf16[2,2,256,2048]{3,2,0,1:T(8,128)(2,1)S(1)}, bf16[2,2,256,2048]{3,2,0,1:T(8,128)(2,1)}, u32[]{:S(2)}) copy-start(bf16[2,2,256,2048]{3,2,0,1:T(8,128)(2,1)} %all-gather.10.cloned.1.call-done) | copy-start | bytes 12582916
  307.8 331.1 %all-gather.14.cloned.1.call-start = ((), (), s32[]{:S(2)}) async-start(), calls=%async_computation.5 | async-start | bytes 9437184 | tf_op jit(solution)/shard_map/all_gather | solution.py:81
  432.4 10.8 copy-start.10
  460.5 8.4 copy-start.4
  468.9 1.0 copy-start.6
  509.3 1.0 copy-start.2
  513.1 197.1 %all-gather.16.cloned.1.call-start = ((), (), s32[]{:S(2)}) async-start(), calls=%async_computation.6 | async-start | bytes 5242880 | tf_op jit(solution)/shard_map/all_gather | solution.py:84
  638.9 11.0 copy-start.12
  677.3 138.0 %all-gather.18.cloned.1.call-start = ((), (), s32[]{:S(2)}) async-start(), calls=%async_computation.7 | async-start | bytes 5242880 | tf_op jit(solution)/shard_map/all_gather | solution.py:87
  710.1 18.5 %copy-start.16 = (bf16[2,2,256,2048]{2,3,0,1:T(8,128)(2,1)S(1)}, bf16[2,2,256,2048]{2,3,0,1:T(8,128)(2,1)}, u32[]{:S(2)}) copy-start(bf16[2,2,256,2048]{2,3,0,1:T(8,128)(2,1)} %all-gather.16.cloned.1.call-done) | copy-start | bytes 12582916
  780.8 102.7 %reduce-scatter.5.cloned.1.call-start = ((), (), s32[]{:S(2)}) async-start(), calls=%async_computation.8 | async-start | bytes 5242880 | tf_op jit(solution)/shard_map/reduce_scatter | solution.py:104
  815.4 4.2 copy-start.14
  815.4 7.8 slice-start
  819.6 3.8 slice-start.1
  838.9 81.7 %all-gather.20.cloned.1.call-start = ((), (), s32[]{:S(2)}) async-start(), calls=%async_computation.9 | async-start | bytes 5242880 | tf_op jit(solution)/shard_map/all_gather | solution.py:109
  886.0 228.3 %all-gather.22.cloned.1.call-start = ((), (), s32[]{:S(2)}) async-start(), calls=%async_computation.10 | async-start | bytes 9437184 | tf_op jit(solution)/shard_map/all_gather | solution.py:111
  920.6 17.6 %copy-start.15 = (bf16[2,2,256,2048]{3,2,0,1:T(8,128)(2,1)S(1)}, bf16[2,2,256,2048]{3,2,0,1:T(8,128)(2,1)}, u32[]{:S(2)}) copy-start(bf16[2,2,256,2048]{3,2,0,1:T(8,128)(2,1)} %all-gather.20.cloned.1.call-done) | copy-start | bytes 12582916
  1114.3 10.8 copy-start.11
  1142.2 8.5 copy-start.8
  1142.2 8.5 copy-start.3
  1142.2 8.5 copy-start.5
  1142.2 8.5 copy-start.7
  1150.7 1.0 copy-start.9
Sparse Core Ops, SparseCore 0:
  10.1 127.1 all-gather.23
  160.6 42.5 reduce-scatter.2
  205.8 34.4 all-gather.9
  307.9 124.4 all-gather.11
  513.2 125.6 all-gather.13
  677.5 32.6 all-gather.15
  780.9 34.4 all-gather.17
  839.0 44.3 reduce-scatter.4
  886.1 34.4 all-gather.19
  988.8 125.4 all-gather.21
